TPU v7x, 32 devices: a whole 2x2x4 slice. The times are simulated.
32 devices in a mesh: comm: 4 (over z), arc: 8 (over y, x, core).
Axes of the slice: x: 2, y: 2, z: 4, core: 2. Of those that a mesh axis runs over, the one named last changes fastest.
Arguments:
- prev_dist: float32 [512, 2048], P('comm', 'arc'), may hold values from 0 to 4
- source_node: int32 [512], P('comm'), may hold values from 0 to 2047, as said below
- arc_tail: int32 [16, 2048], P(None, 'arc'), may hold values from 0 to 2047, as said below
- base_cost: float32 [16, 2048], P(None, 'arc'), may hold values from 0.05 to 1
- arc_price: float32 [16, 2048], P(None, 'arc'), may hold values from 0 to 1
- capacity: float32 [16, 2048], P(None, 'arc')
- path_arcs: int32 [512, 128], P(('comm', 'arc')), may hold values from 0 to 32767, as said below
- demand: float32 [512], P(('comm', 'arc')), may hold values from 0.5 to 2
Outputs:
- final_dist: float32 [512, 2048], P('comm', 'arc')
- new_price: float32 [16, 2048], P(None, 'arc')
Inputs may be any that keep to these rules, and one draw needn't show every extreme that they name: `arc_tail`: the tail of arc s * 2048 + v lies in a node block (nodes 128 b to 128 b + 127) at most 2 blocks before or after v's block, counted around the cycle of blocks. Row k is a walk: the head of path_arcs[k, h + 1] (its id modulo 2048) is the tail of path_arcs[k, h]. `source_node`: the tail of path_arcs[k, 127].
All inputs are finite; a program needn't handle non-finite values.
Results may differ from a plain program's by a relative error of at most 0.00002.
Values sent between devices are 32-bit elements; how exact they have to be, the bound alone decides.
A program may use at most 64 MiB of HBM per device.

v0:
```python
import functools

import jax
import jax.numpy as jnp
from jax import lax
from jax.experimental import pallas as pl
from jax.experimental.pallas import tpu as pltpu
from jax.sharding import PartitionSpec as P

SWEEPS = 8
LANES = 128
REACH = 2
UNROLL = 4

step_size = 0.25
eps_value = 1e-06
MESH_ID = pl.DeviceIdType.MESH


def kernel(A, C, m,
           source_ref, demand_ref, dist_ref, tail_ref, cost_ref, price_ref, cap_ref, path_ref,
           out_ref, newp_ref,
           D, T, W, CODE, F, RF, G, Q,
           d_s, d_r, t_s, t_r, w_s, w_r, f_s, f_r, g_s, g_r, q_s, q_r, o_s, o_r):
    rows = D.shape[2]
    degree, span = tail_ref.shape
    NB = A * m
    node_count = NB * LANES
    me = lax.axis_index("arc")
    mc = lax.axis_index("comm")

    def arc_dev(i):
        return lax.rem(me + i, A)

    def comm_dev(i):
        return lax.rem(mc + i, C)

    W[me] = cost_ref[...] + price_ref[...]
    T[me] = tail_ref[...]
    D[0, me] = dist_ref[me]

    barrier = pltpu.get_barrier_semaphore()
    for i in range(1, A):
        pl.semaphore_signal(barrier, inc=1, device_id=(mc, arc_dev(i)), device_id_type=MESH_ID)
    for i in range(1, C):
        pl.semaphore_signal(barrier, inc=1, device_id=(comm_dev(i), me), device_id_type=MESH_ID)
    pl.semaphore_wait(barrier, A - 1 + C - 1)

    def send(src, dst, ss, rs, dev):
        return pltpu.make_async_remote_copy(src_ref=src, dst_ref=dst, send_sem=ss, recv_sem=rs,
                                            device_id=dev, device_id_type=MESH_ID)

    bulk = []
    for i in range(1, A):
        j = arc_dev(i)
        dev = (mc, j)
        bulk.append(send(tail_ref, T.at[me], t_s.at[i - 1], t_r.at[i - 1], dev))
        bulk.append(send(dist_ref.at[j], D.at[0, me], d_s.at[i - 1], d_r.at[i - 1], dev))
        bulk.append(send(W.at[me], W.at[me], w_s.at[i - 1], w_r.at[i - 1], dev))
    for c in bulk:
        c.start()

    total_rows = NB * degree
    shift_nodes = (node_count - 1).bit_length()
    assert 1 << shift_nodes == node_count
    path = path_ref[...]
    slot_of = path >> shift_nodes
    node_of = path & (node_count - 1)
    row_of = (node_of >> 7) * degree + slot_of
    lane_of = node_of & (LANES - 1)
    row_iota = lax.broadcasted_iota(jnp.int32, (total_rows, LANES), 0)
    lane_iota = lax.broadcasted_iota(jnp.int32, (LANES, LANES), 0)
    acc = jnp.zeros((total_rows, LANES), jnp.float32)
    for k in range(path.shape[0]):
        hi = jnp.where(row_iota == row_of[k:k + 1, :], 1.0, 0.0).astype(jnp.bfloat16)
        lo = jnp.where(lane_iota == lane_of[k:k + 1, :], 1.0, 0.0).astype(jnp.bfloat16)
        count = lax.dot_general(hi, lo, (((1,), (1,)), ((), ())), preferred_element_type=jnp.float32)
        acc = acc + count * demand_ref[k]
    F[...] = acc.reshape(F.shape)

    for c in bulk:
        c.wait_recv()

    sub_iota = lax.broadcasted_iota(jnp.int32, (rows, LANES), 0)
    lane_row = lax.broadcasted_iota(jnp.int32, (rows, LANES), 1)
    source = jnp.zeros((rows, LANES), jnp.int32)
    for r in range(rows):
        source = jnp.where(sub_iota == r, source_ref[me * rows + r], source)
    def prepare(j, _):
        for h in range(m):
            lanes = slice(h * LANES, (h + 1) * LANES)
            vb = j * m + h
            D[0, j, :, lanes] = jnp.where(lane_row + vb * LANES == source, 0.0, D[0, j, :, lanes])
            tail = T[j, :, lanes]
            rel = (tail >> 7) - vb + REACH
            rel = jnp.where(rel < 0, rel + NB, rel)
            rel = jnp.where(rel >= NB, rel - NB, rel)
            CODE[j, :, lanes] = rel
            T[j, :, lanes] = tail & (LANES - 1)
        return 0

    for c in bulk:
        c.wait_send()
    lax.fori_loop(0, A, prepare, 0)

    flows = []
    for i in range(1, A):
        j = arc_dev(i)
        flows.append(send(F.at[j], RF.at[me], f_s.at[i - 1], f_r.at[i - 1], (mc, j)))
    for c in flows:
        c.start()

    sub8 = lax.broadcasted_iota(jnp.int32, (8, LANES), 0)
    halves = [(sub8 & d) == 0 for d in (4, 2, 1)]

    def min_over_slots(parts):
        parts = parts + [parts[-1]] * (8 - len(parts))
        for mask, d in zip(halves, (4, 2, 1)):
            merged = []
            for lower, upper in zip(parts[:d], parts[d:]):
                kept = jnp.where(mask, lower, upper)
                other = jnp.where(mask, upper, lower)
                moved = pltpu.roll(other, d, 0)
                if d != 4:
                    moved = jnp.where(mask, pltpu.roll(other, 8 - d, 0), moved)
                merged.append(jnp.minimum(kept, moved))
            parts = merged
        return parts[0]

    def relax_block(read, write, j, pending):
        for h in range(m):
            lanes = slice(h * LANES, (h + 1) * LANES)
            where_from = []
            for off in range(-REACH, REACH + 1):
                q = h + off
                blk = q % m
                where_from.append((lax.rem(j + (q // m) % A, A), slice(blk * LANES, (blk + 1) * LANES)))
            groups = [slice(g, g + 8) for g in range(0, degree, 8)]
            idx = [T[j, g, lanes] for g in groups]
            weight = [W[j, g, lanes] for g in groups]
            code = [CODE[j, g, lanes] for g in groups]
            masks = [[c == b for b in range(2 * REACH)] for c in code]
            for n, first in enumerate(range(0, rows, 8)):
                last = min(first + 8, rows)
                got = {}
                order = range(len(groups)) if n % 2 == 0 else range(len(groups) - 1, -1, -1)
                for g in order:
                    for r in range(first, last):
                        got[g, r] = [jnp.take_along_axis(
                            jnp.broadcast_to(D[read, jj, r:r + 1, bl], (8, LANES)), idx[g],
                            axis=1, mode="promise_in_bounds") for jj, bl in where_from]
                old = D[read, j, first:last, lanes]
                if pending:
                    pending.pop()()

                def finish(got=got, order=order, masks=masks, weight=weight, first=first, last=last,
                           old=old, j=j, lanes=lanes):
                    cand = {}
                    for g in order:
                        for r in range(first, last):
                            pick = got[g, r][2 * REACH]
                            for b in range(2 * REACH):
                                pick = jnp.where(masks[g][b], got[g, r][b], pick)
                            pick = pick + weight[g]
                            cand[r] = jnp.minimum(cand[r], pick) if r in cand else pick
                    best = min_over_slots([cand[r] for r in range(first, last)])[:last - first]
                    D[write, j, first:last, lanes] = jnp.minimum(old, best)

                pending.append(finish)

    def sweeps(first, last):
        def one(t, _):
            read = lax.rem(t, 2)
            def blk(jo, _):
                pending = []
                for u in range(UNROLL):
                    relax_block(read, 1 - read, jo * UNROLL + u, pending)
                pending.pop()()
                return 0
            assert A % UNROLL == 0
            lax.fori_loop(0, A // UNROLL, blk, 0)
            return 0
        lax.fori_loop(first, last, one, 0)

    sweeps(0, 2)
    for c in flows:
        c.wait()
    total = F[me]
    for i in range(1, A):
        total = total + RF[arc_dev(i)]
    G[mc] = total
    sweeps(2, 3)
    groups = [send(G.at[mc], G.at[mc], g_s.at[i - 1], g_r.at[i - 1], (comm_dev(i), me)) for i in range(1, C)]
    for c in groups:
        c.start()
    sweeps(3, 5)
    for c in groups:
        c.wait()
    flow = G[0]
    for i in range(1, C):
        flow = flow + G[i]
    gradient = [flow[h * degree:(h + 1) * degree, :] - cap_ref[:, h * LANES:(h + 1) * LANES] for h in range(m)]
    square = sum(g * g for g in gradient)
    Q[me] = square
    sweeps(5, 6)
    norms = [send(Q.at[me], Q.at[me], q_s.at[i - 1], q_r.at[i - 1], (mc, arc_dev(i))) for i in range(1, A)]
    for c in norms:
        c.start()
    sweeps(6, SWEEPS - 1)
    for c in norms:
        c.wait()
    square = Q[0]
    for i in range(1, A):
        square = square + Q[i]
    scale_root = jnp.sqrt(jnp.sum(square) / (degree * node_count) + eps_value)
    for h in range(m):
        lanes = slice(h * LANES, (h + 1) * LANES)
        newp_ref[:, lanes] = jnp.maximum(price_ref[:, lanes] + step_size * gradient[h] / scale_root, 0.0)

    read = (SWEEPS - 1) % 2
    outs = [send(D.at[1 - read, arc_dev(i)], out_ref.at[me], o_s.at[i - 1], o_r.at[i - 1], (mc, arc_dev(i)))
            for i in range(1, A)]
    for i in range(1, A + 1):
        pending = []
        relax_block(read, 1 - read, arc_dev(i), pending)
        pending.pop()()
        if i >= 2:
            outs[i - 2].start()
    out_ref[me] = D[1 - read, me]
    for c in outs:
        c.wait()


def shards(A, C, prev_dist, source_node, arc_tail, base_cost, arc_price, capacity, path_arcs, demand):
    commodities, span = prev_dist.shape
    degree = arc_tail.shape[0]
    rows = commodities // A
    m = span // LANES
    f32 = jnp.float32
    vmem = pl.BlockSpec(memory_space=pltpu.VMEM)
    smem = pl.BlockSpec(memory_space=pltpu.SMEM)
    sems = pltpu.SemaphoreType.DMA
    out, new_price = pl.pallas_call(
        functools.partial(kernel, A, C, m),
        out_shape=(jax.ShapeDtypeStruct((A, rows, span), f32), jax.ShapeDtypeStruct((degree, span), f32)),
        in_specs=[smem, smem] + [vmem] * 6,
        out_specs=(vmem, vmem),
        scratch_shapes=[
            pltpu.VMEM((2, A, rows, span), f32),
            pltpu.VMEM((A, degree, span), jnp.int32),
            pltpu.VMEM((A, degree, span), f32),
            pltpu.VMEM((A, degree, span), jnp.int32),
            pltpu.VMEM((A, m * degree, LANES), f32),
            pltpu.VMEM((A, m * degree, LANES), f32),
            pltpu.VMEM((C, m * degree, LANES), f32),
            pltpu.VMEM((A, degree, LANES), f32),
        ] + [sems((A - 1,))] * 8 + [sems((C - 1,))] * 2 + [sems((A - 1,))] * 4,
        compiler_params=pltpu.CompilerParams(collective_id=0, has_side_effects=True),
    )(source_node, demand, prev_dist.reshape(A, rows, span), arc_tail, base_cost, arc_price, capacity, path_arcs)
    return (out.reshape(commodities, span), new_price)


def solution(mesh):
    in_specs = (
        P("comm", "arc"),
        P("comm"),
        P(None, "arc"),
        P(None, "arc"),
        P(None, "arc"),
        P(None, "arc"),
        P(("comm", "arc"), None),
        P(("comm", "arc")),
    )
    out_specs = (P("comm", "arc"), P(None, "arc"))
    body = functools.partial(shards, mesh.shape["arc"], mesh.shape["comm"])
    return jax.shard_map(body, mesh=mesh, in_specs=in_specs, out_specs=out_specs, check_vma=False)
```

profile of v0, /device:TPU:0, one launch (start us, length us, event | category | flops | bytes accessed | tf_op | source)
XLA Modules:
  0.0 47.4 jit_solution(5294641680146023384)
XLA Ops:
  0.6 44.6 %shard_map.95 = (f32[8,16,256]{2,1,0:T(8,128)}, f32[16,256]{1,0:T(8,128)}) custom-call(s32[128]{0:T(128)} %source_ref.1, f32[16]{0:T(128)} %demand_ref.1, f32[8,16,256]{2,1,0:T(8,128)} %bitcast.2, s32[16,256]{1,0:T(8,128)} %tail_ref.1, f32[16,256]{1,0:T(8,128)} %cost_ref.1, f32[16,256]{1,0:T(8,128)} %price_ref.1, f32[16,256]{1,0:T(8,128)} %cap_ref.1, ...), custom_call_target="tpu_custom_call" | custom-call | tf_op jit(solution)/shard_map/pallas_call | solution.py:243
  45.2 0.0 copy-start
  45.2 1.6 %copy.12 = f32[128,256]{1,0:T(8,128)} copy(f32[128,256]{1,0:T(8,128)} %bitcast.3) | data formatting | bytes 262144
  46.8 0.0 copy-done
  46.8 0.6 %copy.13 = f32[16,256]{1,0:T(8,128)} copy(f32[16,256]{1,0:T(8,128)S(1)} %copy-done) | data formatting | bytes 32768
Async XLA Ops:
  45.2 1.6 %copy-start = (f32[16,256]{1,0:T(8,128)S(1)}, f32[16,256]{1,0:T(8,128)}, u32[]{:S(2)}) copy-start(f32[16,256]{1,0:T(8,128)} %get-tuple-element.9) | copy-start | bytes 49156
where the time goes:
time: 47.6 us; the launch traced here: 47.4 us
  Pallas kernels  44.6 us (94%)
  local copies, waits for them, and re-layouts  2.18 us (5%)
  between operations  0.65 us (1%)
    pallas_call x1, Pallas kernels, shards(): pl.pallas_call(functools.partial(kernel, A, C, m), out_shape=(jax.ShapeDt...  44.6 us
    unnamed x4, local copies, waits for them, and re-layouts  2.18 us

commit v1 on v0

v1 whole, which is shorter than its diff:
```python
import functools

import jax
import jax.numpy as jnp
from jax import lax
from jax.experimental import pallas as pl
from jax.experimental.pallas import tpu as pltpu
from jax.sharding import PartitionSpec as P

SWEEPS = 8
LANES = 128
REACH = 2
OFFS = 2 * REACH + 1
PAD = 8
FIXED = 8
BUCKETS = (3, 6, 9, 12, 18)

step_size = 0.25
eps_value = 1e-06
MESH_ID = pl.DeviceIdType.MESH


def send(src, dst, ss, rs, dev):
    return pltpu.make_async_remote_copy(src_ref=src, dst_ref=dst, send_sem=ss, recv_sem=rs,
                                        device_id=dev, device_id_type=MESH_ID)


def flip(index, bits, size):
    return sum(lax.rem(index // b + (bits // b) % 2, 2) * b for b in (1 << n for n in range((size - 1).bit_length())))


def others(A, me):
    chips = A // 2
    assert chips & (chips - 1) == 0
    far = sorted(range(1, chips), key=lambda bits: -bits.bit_count())
    core = lax.rem(me, 2)
    out = [2 * flip(me // 2, bits, chips) + lax.rem(core + c, 2) for bits in far for c in (0, 1)]
    return out + [2 * (me // 2) + 1 - core]


def greet(A, C, me, mc, along_comm):
    barrier = pltpu.get_barrier_semaphore()
    for i in range(1, A):
        pl.semaphore_signal(barrier, inc=1, device_id=(mc, lax.rem(me + i, A)), device_id_type=MESH_ID)
    for i in range(1, C if along_comm else 1):
        pl.semaphore_signal(barrier, inc=1, device_id=(lax.rem(mc + i, C), me), device_id_type=MESH_ID)
    return lambda: pl.semaphore_wait(barrier, A - 1 + (C - 1 if along_comm else 0))


def gather_kernel(A, C, m,
                  source_ref, demand_ref, dist_hbm, tail_hbm, cost_hbm, price_hbm, cap_hbm, path_hbm,
                  X0, KT, WW, COUNT, PI, PW, grad_ref, price_ref,
                  D, dist_ref, tail_ref, cost_ref, cap_ref, path_ref,
                  T, W, F, RF, G,
                  in_s, d_s, d_r, t_s, t_r, w_s, w_r, f_s, f_r, g_s, g_r):
    degree, span = tail_ref.shape
    NB = A * m
    chips = A // 2
    node_count = NB * LANES
    groups = NB // 8
    me = lax.axis_index("arc")
    mc = lax.axis_index("comm")
    chip, core = me // 2, lax.rem(me, 2)
    twin = 2 * chip + 1 - core
    block_lanes = [slice(h * LANES, (h + 1) * LANES) for h in range(m)]

    pairs = ((path_hbm, path_ref), (tail_hbm, tail_ref), (cost_hbm, cost_ref), (price_hbm, price_ref),
             (dist_hbm, dist_ref), (cap_hbm, cap_ref))
    loads = [pltpu.make_async_copy(src, dst, in_s.at[i]) for i, (src, dst) in enumerate(pairs)]
    for c in loads:
        c.start()
    wait_peers = greet(A, C, me, mc, True)
    loads[0].wait()

    total_rows = NB * degree
    shift_nodes = (node_count - 1).bit_length()
    assert 1 << shift_nodes == node_count
    path = path_ref[...]
    slot_of = path >> shift_nodes
    node_of = path & (node_count - 1)
    row_of = (node_of >> 7) * degree + slot_of
    lane_of = node_of & (LANES - 1)
    row_iota = lax.broadcasted_iota(jnp.int32, (total_rows, LANES), 0)
    lane_iota = lax.broadcasted_iota(jnp.int32, (LANES, LANES), 0)
    acc = jnp.zeros((total_rows, LANES), jnp.float32)
    for k in range(path.shape[0]):
        hi = jnp.where(row_iota == row_of[k:k + 1, :], 1.0, 0.0).astype(jnp.bfloat16)
        lo = jnp.where(lane_iota == lane_of[k:k + 1, :], 1.0, 0.0).astype(jnp.bfloat16)
        count = lax.dot_general(hi, lo, (((1,), (1,)), ((), ())), preferred_element_type=jnp.float32)
        acc = acc + count * demand_ref[k]
    F[...] = acc.reshape(F.shape)

    for c in loads[1:]:
        c.wait()
    for h in range(m):
        W[me * m + h] = cost_ref[:, block_lanes[h]] + price_ref[:, block_lanes[h]]
        T[me * m + h] = tail_ref[:, block_lanes[h]]
        D[me * m + h] = dist_ref[me, :, block_lanes[h]]
    wait_peers()

    def share(owner, n, dev):
        at = pl.ds(owner * m, m)
        return [send(T.at[at], T.at[at], t_s.at[n], t_r.at[n], dev),
                send(W.at[at], W.at[at], w_s.at[n], w_r.at[n], dev)]

    flows, dists = [], []
    for i, j in enumerate(others(A, me), 1):
        flows.append(send(F.at[j], RF.at[me], f_s.at[i - 1], f_r.at[i - 1], (mc, j)))
        for h in range(m):
            n = (i - 1) * m + h
            dists.append(send(dist_ref.at[j, :, block_lanes[h]], D.at[me * m + h], d_s.at[n], d_r.at[n], (mc, j)))
    far = []
    for i in range(1, chips):
        far += share(me, i - 1, (mc, 2 * flip(chip, i, chips) + core))
    near = share(me, chips - 1, (mc, twin))
    for c in flows + far + near + dists:
        c.start()
    passed = []
    for i in range(1, chips):
        for c in far[2 * (i - 1):2 * i]:
            c.wait()
        owner = 2 * flip(chip, i, chips) + core
        onward = share(owner, chips - 1 + i, (mc, twin))
        for c in onward:
            c.start()
        passed += onward

    for c in flows:
        c.wait()
    total = F[me]
    for i in range(1, A):
        total = total + RF[lax.rem(me + i, A)]
    G[mc] = total
    shares = [send(G.at[mc], G.at[mc], g_s.at[i - 1], g_r.at[i - 1], (lax.rem(mc + i, C), me)) for i in range(1, C)]
    for c in shares:
        c.start()
    for c in near + passed:
        c.wait()

    sub = lax.broadcasted_iota(jnp.int32, (8, LANES), 0)
    for g in range(groups):
        count = [jnp.zeros((8, LANES), jnp.int32)] * OFFS
        for s in range(degree):
            tail = T[8 * g:8 * g + 8, s, :]
            rel = (tail >> 7) - (8 * g + sub) + REACH
            rel = jnp.where(rel < 0, rel + NB, rel)
            rel = jnp.where(rel >= NB, rel - NB, rel)
            rank = count[0]
            for o in range(1, OFFS):
                rank = jnp.where(rel == o, count[o], rank)
            count = [c + jnp.where(rel == o, 1, 0) for o, c in enumerate(count)]
            KT[g, s] = ((rel * degree + rank) << 7) + (tail & (LANES - 1))
            WW[g, s] = W[8 * g:8 * g + 8, s, :]
        for o in range(OFFS):
            COUNT[g, o] = count[o]

    def build(p, _):
        key = lax.div(p, FIXED) * degree + lax.rem(p, FIXED)
        for g in range(groups):
            PI[g, p], PW[g, p] = arc_of(KT, WW, g, key, degree)
        return 0

    lax.fori_loop(0, OFFS * FIXED, build, 0)

    for c in dists:
        c.wait()
    lane = lax.broadcasted_iota(jnp.int32, (8, LANES), 1)
    for g in range(groups):
        node = (8 * g + sub) * LANES + lane
        for k in range(D.shape[1]):
            old = D[8 * g:8 * g + 8, k, :]
            put(X0.at[k], g, groups, jnp.where(node == source_ref[me * D.shape[1] + k], 0.0, old))
    for c in shares:
        c.wait()
    flow = G[0]
    for i in range(1, C):
        flow = flow + G[i]
    for h in range(m):
        grad_ref[h * degree:(h + 1) * degree, :] = flow[h * degree:(h + 1) * degree, :] - cap_ref[:, block_lanes[h]]


def arc_of(KT, WW, g, key, degree):
    kept = jnp.zeros((8, LANES), jnp.int32)
    weight = jnp.full((8, LANES), jnp.inf, jnp.float32)
    for s in range(degree):
        kt = KT[g, s]
        hit = (kt >> 7) == key
        kept = jnp.where(hit, kt, kept)
        weight = jnp.where(hit, WW[g, s], weight)
    return kept & (LANES - 1), weight


def put(row, g, groups, value):
    row[PAD + 8 * g:PAD + 8 * g + 8, :] = value
    if g == 0:
        row[PAD + 8 * groups:PAD + 8 * groups + REACH, :] = value[:REACH]
    if g == groups - 1:
        row[PAD - REACH:PAD, :] = value[8 - REACH:]


def sweep_kernel(X0, KT, WW, COUNT, PI, PW, Y, X, EI, EW, OFF):
    rows = X0.shape[0]
    groups, degree = KT.shape[:2]

    counts = [[jnp.max(COUNT[g, o]) for o in range(OFFS)] for g in range(groups)]
    for g in range(groups):
        for k in range(rows):
            put(X.at[0, k], g, groups, X0[k, PAD + 8 * g:PAD + 8 * g + 8, :])

    ends = []
    for g in range(groups):
        pos = 0
        for o in range(OFFS):
            def build(i, pos, g=g, o=o):
                EI[g, pos], EW[g, pos] = arc_of(KT, WW, g, o * degree + i, degree)
                OFF[g, pos] = o
                return pos + 1
            pos = lax.fori_loop(FIXED, counts[g][o], build, pos)
        ends.append(pos)
    most = functools.reduce(jnp.maximum, ends)
    sizes = BUCKETS + (OFFS * (degree - FIXED),)
    room = sizes[-1]
    for size in reversed(sizes[:-1]):
        room = jnp.where(most <= size, size, room)

    for g in range(groups):
        def fill(p, _, g=g):
            EI[g, p] = jnp.zeros((8, LANES), jnp.int32)
            EW[g, p] = jnp.full((8, LANES), jnp.inf, jnp.float32)
            OFF[g, p] = 0
            return 0
        lax.fori_loop(ends[g], room, fill, 0)

    def sweep(extra, t):
        read = lax.rem(t, 2)
        for g in range(groups):
            base = PAD + 8 * g - REACH
            best = [X[read, k, PAD + 8 * g:PAD + 8 * g + 8, :] for k in range(rows)]
            todo = [(o + base, PI, PW, o * FIXED + i) for o in range(OFFS) for i in range(FIXED)]
            todo += [(OFF[g, p] + base, EI, EW, p) for p in range(extra)]
            for start, index, weight, p in todo:
                idx = index[g, p]
                w = weight[g, p]
                for k in range(rows):
                    got = jnp.take_along_axis(X[read, k, pl.ds(start, 8), :], idx, axis=1,
                                              mode="promise_in_bounds")
                    best[k] = jnp.minimum(best[k], got + w)
            for k in range(rows):
                put(X.at[1 - read, k], g, groups, best[k])

    for extra in sizes:
        @pl.when(room == extra)
        def _(extra=extra):
            def one(t, _):
                sweep(extra, t)
                return 0
            lax.fori_loop(0, SWEEPS, one, 0)

    for g in range(groups):
        for k in range(rows):
            Y[8 * g:8 * g + 8, k, :] = X[SWEEPS % 2, k, PAD + 8 * g:PAD + 8 * g + 8, :]


def finish_kernel(A, C, m,
                  Y, grad_ref, price_ref,
                  out_ref, newp_ref,
                  Q, o_s, o_r, q_s, q_r):
    degree, span = price_ref.shape
    node_count = A * m * LANES
    me = lax.axis_index("arc")
    mc = lax.axis_index("comm")
    block_lanes = [slice(h * LANES, (h + 1) * LANES) for h in range(m)]

    wait_peers = greet(A, C, me, mc, False)
    gradient = [grad_ref[h * degree:(h + 1) * degree, :] for h in range(m)]
    Q[me] = sum(g * g for g in gradient)
    for h in range(m):
        out_ref[me, :, block_lanes[h]] = Y[me * m + h]
    wait_peers()
    norms, outs = [], []
    for i, j in enumerate(others(A, me), 1):
        norms.append(send(Q.at[me], Q.at[me], q_s.at[i - 1], q_r.at[i - 1], (mc, j)))
        for h in range(m):
            n = (i - 1) * m + h
            outs.append(send(Y.at[j * m + h], out_ref.at[me, :, block_lanes[h]], o_s.at[n], o_r.at[n], (mc, j)))
    for c in norms + outs:
        c.start()
    for c in norms:
        c.wait()
    square = Q[0]
    for i in range(1, A):
        square = square + Q[i]
    scale_root = jnp.sqrt(jnp.sum(square) / (degree * node_count) + eps_value)
    for h in range(m):
        newp_ref[:, block_lanes[h]] = jnp.maximum(
            price_ref[:, block_lanes[h]] + step_size * gradient[h] / scale_root, 0.0)
    for c in outs:
        c.wait()


def store_kernel(out_ref, newp_ref, out_hbm, newp_hbm, sem):
    copies = [pltpu.make_async_copy(out_ref, out_hbm, sem.at[0]), pltpu.make_async_copy(newp_ref, newp_hbm, sem.at[1])]
    for c in copies:
        c.start()
    for c in copies:
        c.wait()


def shards(A, C, prev_dist, source_node, arc_tail, base_cost, arc_price, capacity, path_arcs, demand):
    commodities, span = prev_dist.shape
    degree = arc_tail.shape[0]
    rows = commodities // A
    m = span // LANES
    NB = A * m
    assert NB % 8 == 0 and degree >= FIXED
    f32, i32 = jnp.float32, jnp.int32
    groups = NB // 8
    extras = OFFS * (degree - FIXED)
    vmem = pl.BlockSpec(memory_space=pltpu.VMEM)
    smem = pl.BlockSpec(memory_space=pltpu.SMEM)
    hbm = pl.BlockSpec(memory_space=pltpu.HBM)
    sems = pltpu.SemaphoreType.DMA
    kept_words = (rows * (NB + 2 * PAD) + 16 * groups * degree + 8 * groups * OFFS * (1 + 2 * FIXED)) * LANES
    limit = 64_600_000 - 4 * kept_words
    X0, KT, WW, COUNT, PI, PW, gradient, price = pl.pallas_call(
        functools.partial(gather_kernel, A, C, m),
        out_shape=(pltpu.VMEM((rows, NB + 2 * PAD, LANES), f32), pltpu.VMEM((groups, degree, 8, LANES), i32),
                   pltpu.VMEM((groups, degree, 8, LANES), f32), pltpu.VMEM((groups, OFFS, 8, LANES), i32),
                   pltpu.VMEM((groups, OFFS * FIXED, 8, LANES), i32),
                   pltpu.VMEM((groups, OFFS * FIXED, 8, LANES), f32), pltpu.VMEM((m * degree, LANES), f32),
                   pltpu.VMEM((degree, span), f32)),
        in_specs=[smem] * 2 + [hbm] * 6,
        out_specs=(vmem,) * 8,
        scratch_shapes=[
            pltpu.VMEM((NB, rows, LANES), f32),
            pltpu.VMEM((A, rows, span), f32),
            pltpu.VMEM((degree, span), i32),
            pltpu.VMEM((degree, span), f32),
            pltpu.VMEM((degree, span), f32),
            pltpu.VMEM(path_arcs.shape, i32),
            pltpu.VMEM((NB, degree, LANES), i32),
            pltpu.VMEM((NB, degree, LANES), f32),
            pltpu.VMEM((A, m * degree, LANES), f32),
            pltpu.VMEM((A, m * degree, LANES), f32),
            pltpu.VMEM((C, m * degree, LANES), f32),
        ] + [sems((6,))] + [sems(((A - 1) * m,))] * 2 + [sems((A - 1,))] * 6 + [sems((C - 1,))] * 2,
        compiler_params=pltpu.CompilerParams(collective_id=0, has_side_effects=True, vmem_limit_bytes=limit),
    )(source_node, demand, prev_dist.reshape(A, rows, span), arc_tail, base_cost, arc_price, capacity, path_arcs)
    Y = pl.pallas_call(
        sweep_kernel,
        out_shape=pltpu.VMEM((NB, rows, LANES), f32),
        in_specs=[vmem] * 6,
        out_specs=vmem,
        scratch_shapes=[
            pltpu.VMEM((2, rows, NB + 2 * PAD, LANES), f32),
            pltpu.VMEM((groups, extras, 8, LANES), i32),
            pltpu.VMEM((groups, extras, 8, LANES), f32),
            pltpu.SMEM((groups, extras), i32),
        ],
        compiler_params=pltpu.CompilerParams(vmem_limit_bytes=24 * 2**20),
    )(X0, KT, WW, COUNT, PI, PW)
    out, new_price = pl.pallas_call(
        functools.partial(finish_kernel, A, C, m),
        out_shape=(pltpu.VMEM((A, rows, span), f32), pltpu.VMEM((degree, span), f32)),
        in_specs=[vmem] * 3,
        out_specs=(vmem, vmem),
        scratch_shapes=[pltpu.VMEM((A, degree, LANES), f32)] + [sems(((A - 1) * m,))] * 2 + [sems((A - 1,))] * 2,
        compiler_params=pltpu.CompilerParams(collective_id=1, has_side_effects=True, vmem_limit_bytes=24 * 2**20),
    )(Y, gradient, price)
    out, new_price = pl.pallas_call(
        store_kernel,
        out_shape=(jax.ShapeDtypeStruct(out.shape, f32), jax.ShapeDtypeStruct(new_price.shape, f32)),
        in_specs=[vmem] * 2,
        out_specs=(hbm, hbm),
        scratch_shapes=[sems((2,))],
        compiler_params=pltpu.CompilerParams(vmem_limit_bytes=24 * 2**20),
    )(out, new_price)
    return (out.reshape(commodities, span), new_price)


def solution(mesh):
    in_specs = (
        P("comm", "arc"),
        P("comm"),
        P(None, "arc"),
        P(None, "arc"),
        P(None, "arc"),
        P(None, "arc"),
        P(("comm", "arc"), None),
        P(("comm", "arc")),
    )
    out_specs = (P("comm", "arc"), P(None, "arc"))
    body = functools.partial(shards, mesh.shape["arc"], mesh.shape["comm"])
    return jax.shard_map(body, mesh=mesh, in_specs=in_specs, out_specs=out_specs, check_vma=False)
```

time: 47.6 us -> 41.5 us (0.87)
  Pallas kernels: 44.6 us -> 40.4 us
  local copies, waits for them, and re-layouts: 2.18 us -> 0 us
    pallas_call x1 -> x4, Pallas kernels: 44.6 us -> 40.4 us  [the longest x1 17.7 us: shards(): pl.pallas_call(sweep_kernel, out_shape=pltpu.VMEM((NB, rows, LANES), f32)...]
    unnamed x4 -> x0, local copies, waits for them, and re-layouts: 2.18 us -> none
where the time goes in v1:
time: 41.5 us; the launch traced here: 41.2 us
  Pallas kernels  40.4 us (97%)
  between operations  0.82 us (2%)
    pallas_call x1, Pallas kernels, shards(): pl.pallas_call(sweep_kernel, out_shape=pltpu.VMEM((NB, rows, LANES), f32)...  17.7 us
    pallas_call x1, Pallas kernels, shards(): pl.pallas_call(functools.partial(gather_kernel, A, C, m), out_shape=(pltp...  16.1 us
    pallas_call x1, Pallas kernels, shards(): pl.pallas_call(functools.partial(finish_kernel, A, C, m), out_shape=(pltp...  5.94 us

profile of v1, /device:TPU:0, one launch (start us, length us, event | category | flops | bytes accessed | tf_op | source)
XLA Modules:
  0.0 41.2 jit_solution(2219386690162459247)
XLA Ops:
  0.6 16.1 %shard_map.95 = (f32[16,32,128]{2,1,0:T(8,128)S(1)}, s32[2,16,8,128]{3,2,1,0:T(8,128)S(1)}, f32[2,16,8,128]{3,2,1,0:T(8,128)S(1)}, s32[2,5,8,128]{3,2,1,0:T(8,12...) custom-call(s32[128]{0:T(128)} %source_ref.1, ...), custom_call_target="tpu_custom_call" | custom-call | tf_op jit(solution)/shard_map/pallas_call | solution.py:325
  16.8 17.7 %shard_map.96.Y = f32[16,16,128]{2,1,0:T(8,128)S(1)} custom-call(f32[16,32,128]{2,1,0:T(8,128)S(1)} %get-tuple-element.14.X0, s32[2,16,8,128]{3,2,1,0:T(8,128)S(1)} %get-tuple-element.15.KT, f32[2,16,8,128]{3,2,1,0:T(8,128)S(1)} %get-tuple-element.16.WW, s32[2,5,8,128]{3,2,1,0:T(8,128)S(1)} %get-tuple-element.17.COUNT, ...), custom_call_target="tpu_custom_call" | custom-call | tf_op jit(solution)/shard_map/pallas_call | solution.py:349
  34.5 5.9 %shard_map.97 = (f32[8,16,256]{2,1,0:T(8,128)S(1)}, f32[16,256]{1,0:T(8,128)S(1)}) custom-call(f32[16,16,128]{2,1,0:T(8,128)S(1)} %shard_map.96.Y, f32[32,128]{1,0:T(8,128)S(1)} %get-tuple-element.20.grad_ref, f32[16,256]{1,0:T(8,128)S(1)} %get-tuple-element.21.price_ref), custom_call_target="tpu_custom_call" | custom-call | tf_op jit(solution)/shard_map/pallas_call | solution.py:362
  40.4 0.7 %shard_map.98 = (f32[8,16,256]{2,1,0:T(8,128)}, f32[16,256]{1,0:T(8,128)}) custom-call(f32[8,16,256]{2,1,0:T(8,128)S(1)} %get-tuple-element.22.out_ref, f32[16,256]{1,0:T(8,128)S(1)} %get-tuple-element.23.newp_ref), custom_call_target="tpu_custom_call" | custom-call | tf_op jit(solution)/shard_map/pallas_call | solution.py:370

commit v2 on v1

--- a/solution.py
+++ b/solution.py
@@ -12,8 +12,11 @@
 REACH = 2
 OFFS = 2 * REACH + 1
 PAD = 8
-FIXED = 8
-BUCKETS = (3, 6, 9, 12, 18)
+FIXED = 7
+BUCKETS = (2, 5)
+CHUNK = 5
+MEET = 2
+HALF = LANES // 2
 
 step_size = 0.25
 eps_value = 1e-06
@@ -49,10 +52,10 @@
 
 def gather_kernel(A, C, m,
                   source_ref, demand_ref, dist_hbm, tail_hbm, cost_hbm, price_hbm, cap_hbm, path_hbm,
-                  X0, KT, WW, COUNT, PI, PW, grad_ref, price_ref,
-                  D, dist_ref, tail_ref, cost_ref, cap_ref, path_ref,
-                  T, W, F, RF, G,
-                  in_s, d_s, d_r, t_s, t_r, w_s, w_r, f_s, f_r, g_s, g_r):
+                  X0, KT, WW, COUNT, CAP, PI, PW, PV, flow_ref, price_ref, cap_ref,
+                  D, dist_ref, tail_ref, cost_ref, path_ref,
+                  T, W, F, RF,
+                  in_s, d_s, d_r, t_s, t_r, w_s, w_r, f_s, f_r):
     degree, span = tail_ref.shape
     NB = A * m
     chips = A // 2
@@ -69,7 +72,7 @@
     loads = [pltpu.make_async_copy(src, dst, in_s.at[i]) for i, (src, dst) in enumerate(pairs)]
     for c in loads:
         c.start()
-    wait_peers = greet(A, C, me, mc, True)
+    wait_peers = greet(A, C, me, mc, False)
     loads[0].wait()
 
     total_rows = NB * degree
@@ -125,15 +128,6 @@
             c.start()
         passed += onward
 
-    for c in flows:
-        c.wait()
-    total = F[me]
-    for i in range(1, A):
-        total = total + RF[lax.rem(me + i, A)]
-    G[mc] = total
-    shares = [send(G.at[mc], G.at[mc], g_s.at[i - 1], g_r.at[i - 1], (lax.rem(mc + i, C), me)) for i in range(1, C)]
-    for c in shares:
-        c.start()
     for c in near + passed:
         c.wait()
 
@@ -152,15 +146,36 @@
             KT[g, s] = ((rel * degree + rank) << 7) + (tail & (LANES - 1))
             WW[g, s] = W[8 * g:8 * g + 8, s, :]
         for o in range(OFFS):
-            COUNT[g, o] = count[o]
-
-    def build(p, _):
-        key = lax.div(p, FIXED) * degree + lax.rem(p, FIXED)
+            free = FIXED - jnp.minimum(pltpu.roll(count[o], HALF, 1), FIXED)
+            CAP[g, o] = FIXED + free
+            COUNT[g, o] = jnp.maximum(count[o] - FIXED - free, 0)
+
+    def build(o, _):
         for g in range(groups):
-            PI[g, p], PW[g, p] = arc_of(KT, WW, g, key, degree)
+            kts = [KT[g, s] for s in range(degree)]
+            ranks = [(kt >> 7) - o * degree for kt in kts]
+            weights = [WW[g, s] for s in range(degree)]
+
+            def find(rank):
+                kept = jnp.zeros((8, LANES), jnp.int32)
+                weight = jnp.full((8, LANES), jnp.inf, jnp.float32)
+                for s in range(rank, degree):
+                    hit = ranks[s] == rank
+                    kept = jnp.where(hit, kts[s], kept)
+                    weight = jnp.where(hit, weights[s], weight)
+                return kept, weight
+
+            for i in range(FIXED):
+                own_kept, own_weight = find(i)
+                far_kept, far_weight = [pltpu.roll(x, HALF, 1) for x in find(2 * FIXED - 1 - i)]
+                mine = own_weight < jnp.inf
+                p = o * FIXED + i
+                PI[g, p] = jnp.where(mine, own_kept, far_kept) & (LANES - 1)
+                PW[g, p] = own_weight
+                PV[g, p] = jnp.where(mine, jnp.inf, far_weight)
         return 0
 
-    lax.fori_loop(0, OFFS * FIXED, build, 0)
+    lax.fori_loop(0, OFFS, build, 0)
 
     for c in dists:
         c.wait()
@@ -170,13 +185,12 @@
         for k in range(D.shape[1]):
             old = D[8 * g:8 * g + 8, k, :]
             put(X0.at[k], g, groups, jnp.where(node == source_ref[me * D.shape[1] + k], 0.0, old))
-    for c in shares:
-        c.wait()
-    flow = G[0]
-    for i in range(1, C):
-        flow = flow + G[i]
-    for h in range(m):
-        grad_ref[h * degree:(h + 1) * degree, :] = flow[h * degree:(h + 1) * degree, :] - cap_ref[:, block_lanes[h]]
+    for c in flows:
+        c.wait()
+    total = F[me]
+    for i in range(1, A):
+        total = total + RF[lax.rem(me + i, A)]
+    flow_ref[...] = total
 
 
 def arc_of(KT, WW, g, key, degree):
@@ -198,30 +212,28 @@
         row[PAD - REACH:PAD, :] = value[8 - REACH:]
 
 
-def sweep_kernel(X0, KT, WW, COUNT, PI, PW, Y, X, EI, EW, OFF):
-    rows = X0.shape[0]
+def list_kernel(KT, WW, COUNT, CAP, EI, EW, OFF, choice):
     groups, degree = KT.shape[:2]
-
     counts = [[jnp.max(COUNT[g, o]) for o in range(OFFS)] for g in range(groups)]
-    for g in range(groups):
-        for k in range(rows):
-            put(X.at[0, k], g, groups, X0[k, PAD + 8 * g:PAD + 8 * g + 8, :])
-
     ends = []
     for g in range(groups):
         pos = 0
         for o in range(OFFS):
             def build(i, pos, g=g, o=o):
-                EI[g, pos], EW[g, pos] = arc_of(KT, WW, g, o * degree + i, degree)
+                rank = CAP[g, o] + i
+                key = jnp.where(rank < degree, o * degree + rank, -1)
+                EI[g, pos], EW[g, pos] = arc_of(KT, WW, g, key, degree)
                 OFF[g, pos] = o
                 return pos + 1
-            pos = lax.fori_loop(FIXED, counts[g][o], build, pos)
+            pos = lax.fori_loop(0, counts[g][o], build, pos)
         ends.append(pos)
     most = functools.reduce(jnp.maximum, ends)
-    sizes = BUCKETS + (OFFS * (degree - FIXED),)
-    room = sizes[-1]
-    for size in reversed(sizes[:-1]):
+    room = EI.shape[1]
+    which = len(BUCKETS)
+    for n, size in reversed(list(enumerate(BUCKETS))):
         room = jnp.where(most <= size, size, room)
+        which = jnp.where(most <= size, n, which)
+    choice[0] = which
 
     for g in range(groups):
         def fill(p, _, g=g):
@@ -231,60 +243,100 @@
             return 0
         lax.fori_loop(ends[g], room, fill, 0)
 
-    def sweep(extra, t):
+
+def sweep_kernel(A, C, m, extra,
+                 OFF, X0, PI, PW, PV, EI, EW, flow_ref, price_ref, cap_ref,
+                 out_ref, newp_ref,
+                 X, Y, G, Q,
+                 g_s, g_r, q_s, q_r, o_s, o_r):
+    rows = X0.shape[0]
+    groups = PI.shape[0]
+    degree, span = price_ref.shape
+    node_count = A * m * LANES
+    me = lax.axis_index("arc")
+    mc = lax.axis_index("comm")
+    block_lanes = [slice(h * LANES, (h + 1) * LANES) for h in range(m)]
+
+    wait_peers = greet(A, C, me, mc, True)
+    G[mc] = flow_ref[...]
+    for g in range(groups):
+        for k in range(rows):
+            put(X.at[0, k], g, groups, X0[k, PAD + 8 * g:PAD + 8 * g + 8, :])
+
+    shares = [send(G.at[mc], G.at[mc], g_s.at[i - 1], g_r.at[i - 1], (lax.rem(mc + i, C), me)) for i in range(1, C)]
+    norms, outs = [], []
+    for i, j in enumerate(others(A, me), 1):
+        norms.append(send(Q.at[me], Q.at[me], q_s.at[i - 1], q_r.at[i - 1], (mc, j)))
+        for h in range(m):
+            n = (i - 1) * m + h
+            outs.append(send(Y.at[j * m + h], out_ref.at[me, :, block_lanes[h]], o_s.at[n], o_r.at[n], (mc, j)))
+
+    def gradient(h):
+        flow = G[0, h * degree:(h + 1) * degree, :]
+        for i in range(1, C):
+            flow = flow + G[i, h * degree:(h + 1) * degree, :]
+        return flow - cap_ref[:, block_lanes[h]]
+
+    def sweep(t):
         read = lax.rem(t, 2)
         for g in range(groups):
             base = PAD + 8 * g - REACH
-            best = [X[read, k, PAD + 8 * g:PAD + 8 * g + 8, :] for k in range(rows)]
-            todo = [(o + base, PI, PW, o * FIXED + i) for o in range(OFFS) for i in range(FIXED)]
-            todo += [(OFF[g, p] + base, EI, EW, p) for p in range(extra)]
-            for start, index, weight, p in todo:
+
+            def relax(best, other, start, index, weight, second, p):
                 idx = index[g, p]
                 w = weight[g, p]
                 for k in range(rows):
                     got = jnp.take_along_axis(X[read, k, pl.ds(start, 8), :], idx, axis=1,
                                               mode="promise_in_bounds")
                     best[k] = jnp.minimum(best[k], got + w)
+                    if second is not None:
+                        other[k] = jnp.minimum(other[k], got + second[g, p])
+
+            best = [X[read, k, PAD + 8 * g:PAD + 8 * g + 8, :] for k in range(rows)]
+            other = [jnp.full((8, LANES), jnp.inf, jnp.float32)] * rows
+            for o in range(OFFS):
+                for i in range(FIXED):
+                    relax(best, other, o + base, PI, PW, PV, o * FIXED + i)
+            if extra <= CHUNK:
+                for p in range(extra):
+                    relax(best, other, OFF[g, p] + base, EI, EW, None, p)
+            else:
+                def more(c, best):
+                    best = list(best)
+                    for n in range(CHUNK):
+                        relax(best, None, OFF[g, c * CHUNK + n] + base, EI, EW, None, c * CHUNK + n)
+                    return tuple(best)
+                best = lax.fori_loop(0, extra // CHUNK, more, tuple(best))
             for k in range(rows):
-                put(X.at[1 - read, k], g, groups, best[k])
-
-    for extra in sizes:
-        @pl.when(room == extra)
-        def _(extra=extra):
-            def one(t, _):
-                sweep(extra, t)
-                return 0
-            lax.fori_loop(0, SWEEPS, one, 0)
+                put(X.at[1 - read, k], g, groups, jnp.minimum(best[k], pltpu.roll(other[k], HALF, 1)))
+
+    def one(t, _):
+        @pl.when(t == MEET)
+        def _():
+            wait_peers()
+            for c in shares:
+                c.start()
+
+        @pl.when(t == SWEEPS - 1)
+        def _():
+            for c in shares:
+                c.wait()
+            Q[me] = sum(g * g for g in [gradient(h) for h in range(m)])
+            for c in norms:
+                c.start()
+
+        sweep(t)
+        return 0
+
+    lax.fori_loop(0, SWEEPS, one, 0)
 
     for g in range(groups):
         for k in range(rows):
             Y[8 * g:8 * g + 8, k, :] = X[SWEEPS % 2, k, PAD + 8 * g:PAD + 8 * g + 8, :]
-
-
-def finish_kernel(A, C, m,
-                  Y, grad_ref, price_ref,
-                  out_ref, newp_ref,
-                  Q, o_s, o_r, q_s, q_r):
-    degree, span = price_ref.shape
-    node_count = A * m * LANES
-    me = lax.axis_index("arc")
-    mc = lax.axis_index("comm")
-    block_lanes = [slice(h * LANES, (h + 1) * LANES) for h in range(m)]
-
-    wait_peers = greet(A, C, me, mc, False)
-    gradient = [grad_ref[h * degree:(h + 1) * degree, :] for h in range(m)]
-    Q[me] = sum(g * g for g in gradient)
+    for c in outs:
+        c.start()
     for h in range(m):
         out_ref[me, :, block_lanes[h]] = Y[me * m + h]
-    wait_peers()
-    norms, outs = [], []
-    for i, j in enumerate(others(A, me), 1):
-        norms.append(send(Q.at[me], Q.at[me], q_s.at[i - 1], q_r.at[i - 1], (mc, j)))
-        for h in range(m):
-            n = (i - 1) * m + h
-            outs.append(send(Y.at[j * m + h], out_ref.at[me, :, block_lanes[h]], o_s.at[n], o_r.at[n], (mc, j)))
-    for c in norms + outs:
-        c.start()
     for c in norms:
         c.wait()
     square = Q[0]
@@ -293,7 +345,7 @@
     scale_root = jnp.sqrt(jnp.sum(square) / (degree * node_count) + eps_value)
     for h in range(m):
         newp_ref[:, block_lanes[h]] = jnp.maximum(
-            price_ref[:, block_lanes[h]] + step_size * gradient[h] / scale_root, 0.0)
+            price_ref[:, block_lanes[h]] + step_size * gradient(h) / scale_root, 0.0)
     for c in outs:
         c.wait()
 
@@ -304,6 +356,10 @@
         c.start()
     for c in copies:
         c.wait()
+
+
+def extras_of(degree):
+    return OFFS * (degree - FIXED)
 
 
 def shards(A, C, prev_dist, source_node, arc_tail, base_cost, arc_price, capacity, path_arcs, demand):
@@ -312,61 +368,69 @@
     rows = commodities // A
     m = span // LANES
     NB = A * m
-    assert NB % 8 == 0 and degree >= FIXED
+    assert NB % 8 == 0 and degree >= 2 * FIXED and extras_of(degree) % CHUNK == 0
     f32, i32 = jnp.float32, jnp.int32
     groups = NB // 8
-    extras = OFFS * (degree - FIXED)
+    extras = extras_of(degree)
+    pitch = NB + 2 * PAD + (8 if (NB // 8) % 2 == 0 else 0)
     vmem = pl.BlockSpec(memory_space=pltpu.VMEM)
     smem = pl.BlockSpec(memory_space=pltpu.SMEM)
     hbm = pl.BlockSpec(memory_space=pltpu.HBM)
     sems = pltpu.SemaphoreType.DMA
-    kept_words = (rows * (NB + 2 * PAD) + 16 * groups * degree + 8 * groups * OFFS * (1 + 2 * FIXED)) * LANES
+    kept_words = (rows * (NB + 2 * PAD) + 16 * groups * degree + 8 * groups * OFFS * (2 + 3 * FIXED)) * LANES
     limit = 64_600_000 - 4 * kept_words
-    X0, KT, WW, COUNT, PI, PW, gradient, price = pl.pallas_call(
+    X0, KT, WW, COUNT, CAP, PI, PW, PV, flow, price, cap = pl.pallas_call(
         functools.partial(gather_kernel, A, C, m),
         out_shape=(pltpu.VMEM((rows, NB + 2 * PAD, LANES), f32), pltpu.VMEM((groups, degree, 8, LANES), i32),
                    pltpu.VMEM((groups, degree, 8, LANES), f32), pltpu.VMEM((groups, OFFS, 8, LANES), i32),
+                   pltpu.VMEM((groups, OFFS, 8, LANES), i32),
                    pltpu.VMEM((groups, OFFS * FIXED, 8, LANES), i32),
+                   pltpu.VMEM((groups, OFFS * FIXED, 8, LANES), f32),
                    pltpu.VMEM((groups, OFFS * FIXED, 8, LANES), f32), pltpu.VMEM((m * degree, LANES), f32),
-                   pltpu.VMEM((degree, span), f32)),
+                   pltpu.VMEM((degree, span), f32), pltpu.VMEM((degree, span), f32)),
         in_specs=[smem] * 2 + [hbm] * 6,
-        out_specs=(vmem,) * 8,
+        out_specs=(vmem,) * 11,
         scratch_shapes=[
             pltpu.VMEM((NB, rows, LANES), f32),
             pltpu.VMEM((A, rows, span), f32),
             pltpu.VMEM((degree, span), i32),
-            pltpu.VMEM((degree, span), f32),
             pltpu.VMEM((degree, span), f32),
             pltpu.VMEM(path_arcs.shape, i32),
             pltpu.VMEM((NB, degree, LANES), i32),
             pltpu.VMEM((NB, degree, LANES), f32),
             pltpu.VMEM((A, m * degree, LANES), f32),
             pltpu.VMEM((A, m * degree, LANES), f32),
-            pltpu.VMEM((C, m * degree, LANES), f32),
-        ] + [sems((6,))] + [sems(((A - 1) * m,))] * 2 + [sems((A - 1,))] * 6 + [sems((C - 1,))] * 2,
+        ] + [sems((6,))] + [sems(((A - 1) * m,))] * 2 + [sems((A - 1,))] * 6,
         compiler_params=pltpu.CompilerParams(collective_id=0, has_side_effects=True, vmem_limit_bytes=limit),
     )(source_node, demand, prev_dist.reshape(A, rows, span), arc_tail, base_cost, arc_price, capacity, path_arcs)
-    Y = pl.pallas_call(
-        sweep_kernel,
-        out_shape=pltpu.VMEM((NB, rows, LANES), f32),
-        in_specs=[vmem] * 6,
-        out_specs=vmem,
-        scratch_shapes=[
-            pltpu.VMEM((2, rows, NB + 2 * PAD, LANES), f32),
-            pltpu.VMEM((groups, extras, 8, LANES), i32),
-            pltpu.VMEM((groups, extras, 8, LANES), f32),
-            pltpu.SMEM((groups, extras), i32),
-        ],
-        compiler_params=pltpu.CompilerParams(vmem_limit_bytes=24 * 2**20),
-    )(X0, KT, WW, COUNT, PI, PW)
-    out, new_price = pl.pallas_call(
-        functools.partial(finish_kernel, A, C, m),
-        out_shape=(pltpu.VMEM((A, rows, span), f32), pltpu.VMEM((degree, span), f32)),
-        in_specs=[vmem] * 3,
-        out_specs=(vmem, vmem),
-        scratch_shapes=[pltpu.VMEM((A, degree, LANES), f32)] + [sems(((A - 1) * m,))] * 2 + [sems((A - 1,))] * 2,
-        compiler_params=pltpu.CompilerParams(collective_id=1, has_side_effects=True, vmem_limit_bytes=24 * 2**20),
-    )(Y, gradient, price)
+    local = pltpu.CompilerParams(vmem_limit_bytes=24 * 2**20)
+    EI, EW, OFF, choice = pl.pallas_call(
+        list_kernel,
+        out_shape=(pltpu.VMEM((groups, extras, 8, LANES), i32), pltpu.VMEM((groups, extras, 8, LANES), f32),
+                   jax.ShapeDtypeStruct((groups, extras), i32), jax.ShapeDtypeStruct((1,), i32)),
+        in_specs=[vmem] * 4,
+        out_specs=(vmem, vmem, smem, smem),
+        compiler_params=local,
+    )(KT, WW, COUNT, CAP)
+
+    def branch(n, extra):
+        return lambda *operands: pl.pallas_call(
+            functools.partial(sweep_kernel, A, C, m, extra),
+            out_shape=(pltpu.VMEM((A, rows, span), f32), pltpu.VMEM((degree, span), f32)),
+            in_specs=[smem] + [vmem] * 9,
+            out_specs=(vmem, vmem),
+            scratch_shapes=[
+                pltpu.VMEM((2, rows, pitch, LANES), f32),
+                pltpu.VMEM((NB, rows, LANES), f32),
+                pltpu.VMEM((C, m * degree, LANES), f32),
+                pltpu.VMEM((A, degree, LANES), f32),
+            ] + [sems((C - 1,))] * 2 + [sems((A - 1,))] * 2 + [sems(((A - 1) * m,))] * 2,
+            compiler_params=pltpu.CompilerParams(collective_id=1 + n, has_side_effects=True,
+                                                 vmem_limit_bytes=24 * 2**20),
+        )(*operands)
+
+    out, new_price = lax.switch(choice[0], [branch(n, extra) for n, extra in enumerate(BUCKETS + (extras,))],
+                                OFF, X0, PI, PW, PV, EI, EW, flow, price, cap)
     out, new_price = pl.pallas_call(
         store_kernel,
         out_shape=(jax.ShapeDtypeStruct(out.shape, f32), jax.ShapeDtypeStruct(new_price.shape, f32)),

time: 41.5 us -> 35.8 us (0.86)
  Pallas kernels: 40.4 us -> 34.3 us
  between operations: 0.82 us -> 1.31 us
    pallas_call x1, Pallas kernels: 16.1 us -> 12.9 us  [shards(): pl.pallas_call(functools.partial(gather_kernel, A, C, m), out_shape=(pltp...]
    pallas_call x2, Pallas kernels: 23.6 us -> 20.8 us  [the longest x1 19.8 us: branch(): pl.pallas_call(functools.partial(sweep_kernel, A, C, m, extra), out_shape...]
where the time goes in v2:
time: 35.8 us; the launch traced here: 35.7 us
  Pallas kernels  34.3 us (96%)
  between operations  1.31 us (4%)
    pallas_call x1, Pallas kernels, branch(): pl.pallas_call(functools.partial(sweep_kernel, A, C, m, extra), out_shape...  19.8 us
    pallas_call x1, Pallas kernels, shards(): pl.pallas_call(functools.partial(gather_kernel, A, C, m), out_shape=(pltp...  12.9 us
    pallas_call x1, Pallas kernels, shards(): pl.pallas_call(list_kernel, out_shape=(pltpu.VMEM((groups, extras, 8, LAN...  0.98 us

profile of v2, /device:TPU:0, one launch (start us, length us, event | category | flops | bytes accessed | tf_op | source)
XLA Modules:
  0.0 35.7 jit_solution(12711844637508690599)
XLA Ops:
  0.6 12.9 %shard_map.95 = (f32[16,32,128]{2,1,0:T(8,128)S(1)}, s32[2,16,8,128]{3,2,1,0:T(8,128)S(1)}, f32[2,16,8,128]{3,2,1,0:T(8,128)S(1)}, s32[2,5,8,128]{3,2,1,0:T(8,12...) custom-call(s32[128]{0:T(128)} %source_ref.1, ...), custom_call_target="tpu_custom_call" | custom-call | tf_op jit(solution)/shard_map/pallas_call | solution.py:382
  13.5 1.0 %shard_map.96 = (s32[2,45,8,128]{3,2,1,0:T(8,128)S(1)}, f32[2,45,8,128]{3,2,1,0:T(8,128)S(1)}, s32[2,45]{1,0:T(2,128)S(1)}, s32[1]{0:T(128)}) custom-call(s32[2,16,8,128]{3,2,1,0:T(8,128)S(1)} %get-tuple-element.111.KT, f32[2,16,8,128]{3,2,1,0:T(8,128)S(1)} %get-tuple-element.112.WW, s32[2,5,8,128]{3,2,1,0:T(8,128)S(1)} %get-tuple-element.113.COUNT, ...), custom_call_target="tpu_custom_call" | custom-call | tf_op jit(solution)/shard_map/pallas_call | solution.py:407
  15.1 19.8 %conditional.1 = ((f32[8,16,256]{2,1,0:T(8,128)S(1)}, f32[16,256]{1,0:T(8,128)S(1)})) conditional(s32[]{:T(128)} %bitcast.1, (s32[2,45]{1,0:T(2,128)S(1)}, f32[16,32,128]{2,1,0:T(8,128)S(1)}, s32[2,35,8,128]{3,2,1,0:T(8,128)S(1)}, f32[2,35,8,128]{3,2,1,0:T(8,128)S(1)}, f32[2,35,8,128]{3,2,1,0:T(8,128)S(1)}, ...), branch_computations={%region_0.0_spmd, %region_1.0_spmd, %region_2.0_spmd} | conditional | bytes 8 | solution.py:432
  15.2 19.8 %branch_1_fun.1 = (f32[8,16,256]{2,1,0:T(8,128)S(1)}, f32[16,256]{1,0:T(8,128)S(1)}) custom-call(s32[2,45]{1,0:T(2,128)S(1)} %get-tuple-element.70.OFF, f32[16,32,128]{2,1,0:T(8,128)S(1)} %get-tuple-element.71.X0, s32[2,35,8,128]{3,2,1,0:T(8,128)S(1)} %get-tuple-element.72.PI, f32[2,35,8,128]{3,2,1,0:T(8,128)S(1)} %get-tuple-element.73.PW, ...), custom_call_target="tpu_custom_call" | custom-call | tf_op jit(solution)/shard_map/cond/branch_1_fun/pallas_call | solution.py:417
  35.0 0.7 %shard_map.97 = (f32[8,16,256]{2,1,0:T(8,128)}, f32[16,256]{1,0:T(8,128)}) custom-call(f32[8,16,256]{2,1,0:T(8,128)S(1)} %get-tuple-element.126.out_ref, f32[16,256]{1,0:T(8,128)S(1)} %get-tuple-element.127.newp_ref), custom_call_target="tpu_custom_call" | custom-call | tf_op jit(solution)/shard_map/pallas_call | solution.py:434
